TPU v7x, 32 devices: a whole 2x2x4 slice. The times are simulated.
32 devices in a mesh: dp: 2 (over y), expert: 16 (over z, x, core).
Axes of the slice: x: 2, y: 2, z: 4, core: 2. Of those that a mesh axis runs over, the one named last changes fastest.
Arguments:
- tokens: bfloat16 [256, 2880], P(('dp', 'expert')), may hold values from -6 to 6
- routes: int32 [2, 256, 4], P(None, ('dp', 'expert')), may hold values from 0 to 15, all different within a row; in each aligned block of 8 rows (0 to 7, 8 to 15, ..., all dimensions but the last counted through in order) at most 4 rows name the same one
- placement: int32 [2, 16], replicated, may hold values from 0 to 15, each once within a row
- up_weight: bfloat16 [2, 16, 2880, 1440], P(None, 'expert', None, 'dp'), may hold values from -0.109375 to 0.109375
- down_weight: bfloat16 [2, 16, 1440, 2880], P(None, 'expert', 'dp'), may hold values from -0.15625 to 0.15625
- router_weight: bfloat16 [2, 16, 2880], P(None, 'expert'), may hold values from -0.21875 to 0.21875
Outputs:
- final_stream: bfloat16 [256, 2880], P(('dp', 'expert'))
Inputs may be any that keep to these rules, and one draw needn't show every extreme that they name: `routes`: each row names 4 different experts. Within one layer's rows of one device no expert is named by more than 4 rows, and some device names some expert exactly 4 times. `placement`: each layer's row is a permutation of the slots.
All inputs are finite; a program needn't handle non-finite values.
Results may differ from a plain program's by a relative error of at most 0.008.
Values may be sent and summed in bfloat16 or wider, within the bound.
A program may use at most 64 MiB of HBM per device.

v0:
```python
import jax
import jax.numpy as jnp
from jax import lax
from jax.sharding import PartitionSpec as P


def rms_rows(stream):
    values = stream.astype(jnp.float32)
    inverse = lax.rsqrt(jnp.mean(values * values, axis=-1, keepdims=True) + 1e-05)
    return (values * inverse).astype(jnp.bfloat16)


def slot_table(route_rows, place_row, columns, capacity):
    tok_rows, top_k = route_rows.shape
    experts = place_row.shape[0]
    matches = route_rows[:, :, None] == jnp.arange(experts, dtype=jnp.int32)[None, None, :]
    target = jnp.sum(jnp.where(matches, place_row[None, None, :], 0), axis=2).reshape(-1)
    row_count = target.shape[0]
    positions = jnp.arange(row_count, dtype=jnp.int32)
    earlier = (positions[None, :] < positions[:, None]) & (target[None, :] == target[:, None])
    row_rank = jnp.sum(earlier.astype(jnp.int32), axis=1)
    placed = (target[:, None, None] == jnp.arange(columns, dtype=jnp.int32)[None, :, None]) & (
        row_rank[:, None, None] == jnp.arange(capacity, dtype=jnp.int32)[None, None, :]
    )
    slot_map = jnp.sum(
        placed.reshape(tok_rows, top_k, columns, capacity).astype(jnp.float32), axis=1
    )
    return jnp.transpose(slot_map, (1, 2, 0))


def per_device(tokens, routes, placement, up_weight, down_weight, router_weight):
    groups = lax.axis_size("dp")
    columns = lax.axis_size("expert")
    tok_rows = tokens.shape[0]
    top_k = routes.shape[2]
    capacity = 2 * tok_rows * top_k // columns

    def layer_step(stream, packed):
        route_rows, place_row, up_part, down_part, router_part = packed
        normed = rms_rows(stream)
        slot_map = slot_table(route_rows, place_row, columns, capacity)
        outgoing = jnp.einsum(
            "jct,td->jcd", slot_map.astype(jnp.bfloat16), normed, preferred_element_type=jnp.float32
        ).astype(jnp.bfloat16)
        arrived = lax.all_to_all(
            outgoing, "expert", split_axis=0, concat_axis=0, tiled=True
        ).reshape(columns * capacity, -1)
        affinity = jax.nn.sigmoid(
            jnp.dot(arrived, router_part[0], preferred_element_type=jnp.float32)
        ).astype(jnp.bfloat16)
        all_rows, all_gates = (
            lax.all_gather(arrived, "dp", axis=0, tiled=True),
            lax.all_gather(affinity, "dp", axis=0, tiled=True),
        )
        hidden = jax.nn.silu(
            jnp.dot(all_rows, up_part[0], preferred_element_type=jnp.float32)
        ).astype(jnp.bfloat16)
        part_sums = jnp.dot(hidden, down_part[0], preferred_element_type=jnp.float32).astype(
            jnp.bfloat16
        )
        part_sums = part_sums.reshape(groups, columns, capacity, -1)
        all_gates = all_gates.reshape(groups, columns, capacity)
        returned, gates_back = (
            lax.all_to_all(
                lax.all_to_all(part_sums, "dp", split_axis=0, concat_axis=0, tiled=True),
                "expert",
                split_axis=1,
                concat_axis=1,
                tiled=True,
            ),
            lax.all_to_all(
                lax.all_to_all(all_gates, "dp", split_axis=0, concat_axis=0, tiled=True),
                "expert",
                split_axis=1,
                concat_axis=1,
                tiled=True,
            ),
        )
        weights = slot_map * gates_back[0].astype(jnp.float32)[:, :, None]
        numerator = jnp.einsum(
            "ect,gecd->td",
            weights.astype(jnp.bfloat16),
            returned,
            preferred_element_type=jnp.float32,
        )
        denominator = jnp.sum(weights, axis=(0, 1))
        updated = stream.astype(jnp.float32) + numerator / jnp.maximum(denominator, 0.5)[:, None]
        return (updated.astype(jnp.bfloat16), None)

    result_stream, unused = lax.scan(
        layer_step, tokens, (routes, placement, up_weight, down_weight, router_weight)
    )
    return result_stream


def solution(mesh):
    return jax.shard_map(
        per_device,
        mesh=mesh,
        in_specs=(
            P(("dp", "expert"), None),
            P(None, ("dp", "expert"), None),
            P(),
            P(None, "expert", None, "dp"),
            P(None, "expert", "dp", None),
            P(None, "expert", None),
        ),
        out_specs=P(("dp", "expert"), None),
        check_vma=False,
    )
```

profile of v0, /device:TPU:1, one launch (start us, length us, event | category | flops | bytes accessed | tf_op | source)
XLA Modules:
  0.0 197.3 jit_solution(17094374580464921686)
XLA Ops:
  0.0 0.8 copy.73
  0.8 195.9 %while.10 = (s32[]{:T(128)}, bf16[8,2880]{1,0:T(8,128)(2,1)S(1)}, s32[2,8,4]{1,2,0:T(4,128)}, s32[2,16]{1,0:T(2,128)}, bf16[2,1,2880]{2,0,1:T(2,128)(2,1)}, /*in...) while((s32[]{:T(128)}, bf16[8,2880]{1,0:T(8,128)(2,1)S(1)}, ...), condition=%wide.region_7.8_spmd, body=%wide.region_0.7_spmd.sunk | while | flops 1069763072 | bytes 25014808 | solution.py:90
  0.8 0.7 fusion.67
  1.5 0.7 dynamic-slice_bitcast_fusion.2
  2.2 0.2 select_reduce_fusion.2
  2.5 0.1 fusion.66
  2.8 0.2 convert_reduce_fusion.6
  3.2 0.3 convolution_convert_fusion.2
  3.6 0.9 copy.58
  4.4 7.3 %all-to-all-start = ((bf16[16,4,2880]{2,1,0:T(4,128)(2,1)}), bf16[16,4,2880]{2,1,0:T(4,128)(2,1)S(1)}, u32[]{:S(2)}, u32[]{:S(2)}) async-start(bf16[16,4,2880]{2,1,0:T(4,128)(2,1)} %copy.58), calls=%async_computation | async-start | bytes 753664 | tf_op jit(solution)/shard_map/while/body/eval_jaxpr/all_to_all | solution.py:45
  11.8 1.2 dynamic-slice.2
  13.6 9.7 %all-to-all-done = bf16[16,4,2880]{2,1,0:T(4,128)(2,1)S(1)} async-done(((bf16[16,4,2880]{2,1,0:T(4,128)(2,1)}), bf16[16,4,2880]{2,1,0:T(4,128)(2,1)S(1)}, u32[]{:S(2)}, u32[]{:S(2)}) %all-to-all-start) | async-done | bytes 368672 | tf_op jit(solution)/shard_map/while/body/eval_jaxpr/all_to_all | solution.py:45
  23.3 0.2 reshape.105
  23.5 10.6 %all_gather.7 = bf16[128,2880]{1,0:T(8,128)(2,1)S(1)} all-gather(bf16[64,2880]{1,0:T(8,128)(2,1)S(1)} %reshape.105), channel_id=1, replica_groups=mesh['dp'=2,'expert'=16] {'dp'}, dimensions={0}, use_global_device_ids=true | all-gather | bytes 1105920 | tf_op jit(solution)/shard_map/while/body/eval_jaxpr/all_gather | solution.py:52
  34.1 0.9 fusion.69
  35.0 0.3 dynamic-update-slice.2
  35.2 3.8 %all-reduce.2 = bf16[128]{0:T(256)(128)(2,1)S(1)} all-reduce(bf16[128]{0:T(256)(128)(2,1)S(1)} %dynamic-update-slice.2), channel_id=1, replica_groups=mesh['dp'=2,'expert'=16] {'dp'}, use_global_device_ids=true, to_apply=%add | all-reduce | flops 128 | bytes 512 | tf_op jit(solution)/shard_map/while
  39.0 0.1 reshape.107
  39.1 0.7 copy.61
  39.8 3.2 %all-to-all-start.3 = ((bf16[2,16,4]{1,2,0:T(4,128)(2,1)}), bf16[2,16,4]{1,2,0:T(4,128)(2,1)S(1)}, u32[]{:S(2)}, u32[]{:S(2)}) async-start(bf16[2,16,4]{1,2,0:T(4,128)(2,1)} %copy.61), calls=%async_computation.3 | async-start | bytes 4096 | tf_op jit(solution)/shard_map/while/body/eval_jaxpr/all_to_all | solution.py:72
  43.0 8.2 %fusion.68 = bf16[128,2880]{0,1:T(8,128)(2,1)S(1)} fusion(bf16[2,1,720,2880]{3,2,1,0:T(8,128)(2,1)} %get-tuple-element.130, s32[]{:T(128)} %get-tuple-element.112, bf16[128,2880]{1,0:T(8,128)(2,1)S(1)} %all_gather.7, bf16[2,1,2880,720]{2,3,1,0:T(8,128)(2,1)} %get-tuple-element.129), kind=kOutput, calls=%fused_computation.6.clone.1 | convolution fusion | flops 1062512640 | bytes 9954304 | tf_op jit(solution)/shard_map/while/body/eval_jaxpr/dot_general | solution.py:58
  51.3 0.4 copy.59
  51.6 1.1 reshape.106
  52.7 3.5 %all-to-all-start.1 = ((bf16[2,16,4,2880]{3,2,1,0:T(4,128)(2,1)}), bf16[2,16,4,2880]{3,2,1,0:T(4,128)(2,1)S(1)}, u32[]{:S(2)}, u32[]{:S(2)}) async-start(bf16[2,16,4,2880]{3,2,1,0:T(4,128)(2,1)} %reshape.106), calls=%async_computation.1 | async-start | bytes 1507328 | tf_op jit(solution)/shard_map/while/body/eval_jaxpr/all_to_all | solution.py:65
  56.2 0.7 copy.62
  56.9 7.4 %all-to-all-done.1 = bf16[2,16,4,2880]{3,2,1,0:T(4,128)(2,1)S(1)} async-done(((bf16[2,16,4,2880]{3,2,1,0:T(4,128)(2,1)}), bf16[2,16,4,2880]{3,2,1,0:T(4,128)(2,1)S(1)}, u32[]{:S(2)}, u32[]{:S(2)}) %all-to-all-start.1) | async-done | bytes 737312 | tf_op jit(solution)/shard_map/while/body/eval_jaxpr/all_to_all | solution.py:65
  64.3 7.1 %all-to-all-start.4 = ((bf16[2,16,4]{2,0,1:T(2,128)(2,1)}), bf16[2,16,4]{2,0,1:T(2,128)(2,1)S(1)}, u32[]{:S(2)}, u32[]{:S(2)}) async-start(bf16[2,16,4]{2,0,1:T(2,128)(2,1)} %copy.62), calls=%async_computation.4 | async-start | bytes 16384 | tf_op jit(solution)/shard_map/while/body/eval_jaxpr/all_to_all | solution.py:71
  71.4 1.1 copy.60
  72.5 4.6 %all-to-all-done.4 = bf16[2,16,4]{2,0,1:T(2,128)(2,1)S(1)} async-done(((bf16[2,16,4]{2,0,1:T(2,128)(2,1)}), bf16[2,16,4]{2,0,1:T(2,128)(2,1)S(1)}, u32[]{:S(2)}, u32[]{:S(2)}) %all-to-all-start.4) | async-done | bytes 288 | tf_op jit(solution)/shard_map/while/body/eval_jaxpr/all_to_all | solution.py:71
  77.1 4.1 %all-to-all-start.2 = ((bf16[2,16,4,2880]{3,2,0,1:T(4,128)(2,1)}), bf16[2,16,4,2880]{3,2,0,1:T(4,128)(2,1)S(1)}, u32[]{:S(2)}, u32[]{:S(2)}) async-start(bf16[2,16,4,2880]{3,2,0,1:T(4,128)(2,1)} %copy.60), calls=%async_computation.2 | async-start | bytes 1507328 | tf_op jit(solution)/shard_map/while/body/eval_jaxpr/all_to_all | solution.py:64
  81.4 0.1 multiply_reduce_fusion.2
  81.5 17.9 %all-to-all-done.2 = bf16[2,16,4,2880]{3,2,0,1:T(4,128)(2,1)S(1)} async-done(((bf16[2,16,4,2880]{3,2,0,1:T(4,128)(2,1)}), bf16[2,16,4,2880]{3,2,0,1:T(4,128)(2,1)S(1)}, u32[]{:S(2)}, u32[]{:S(2)}) %all-to-all-start.2) | async-done | bytes 737312 | tf_op jit(solution)/shard_map/while/body/eval_jaxpr/all_to_all | solution.py:64
  99.4 0.3 fusion.70
  99.7 0.7 fusion.67
  100.4 0.7 dynamic-slice_bitcast_fusion.2
  101.1 0.2 select_reduce_fusion.2
  101.5 0.1 fusion.66
  101.7 0.2 convert_reduce_fusion.6
  102.2 0.3 convolution_convert_fusion.2
  102.5 0.9 copy.58
  103.4 5.3 %all-to-all-start = ((bf16[16,4,2880]{2,1,0:T(4,128)(2,1)}), bf16[16,4,2880]{2,1,0:T(4,128)(2,1)S(1)}, u32[]{:S(2)}, u32[]{:S(2)}) async-start(bf16[16,4,2880]{2,1,0:T(4,128)(2,1)} %copy.58), calls=%async_computation | async-start | bytes 753664 | tf_op jit(solution)/shard_map/while/body/eval_jaxpr/all_to_all | solution.py:45
  108.7 1.2 dynamic-slice.2
  110.6 9.7 %all-to-all-done = bf16[16,4,2880]{2,1,0:T(4,128)(2,1)S(1)} async-done(((bf16[16,4,2880]{2,1,0:T(4,128)(2,1)}), bf16[16,4,2880]{2,1,0:T(4,128)(2,1)S(1)}, u32[]{:S(2)}, u32[]{:S(2)}) %all-to-all-start) | async-done | bytes 368672 | tf_op jit(solution)/shard_map/while/body/eval_jaxpr/all_to_all | solution.py:45
  120.3 0.2 reshape.105
  120.4 10.6 %all_gather.7 = bf16[128,2880]{1,0:T(8,128)(2,1)S(1)} all-gather(bf16[64,2880]{1,0:T(8,128)(2,1)S(1)} %reshape.105), channel_id=1, replica_groups=mesh['dp'=2,'expert'=16] {'dp'}, dimensions={0}, use_global_device_ids=true | all-gather | bytes 1105920 | tf_op jit(solution)/shard_map/while/body/eval_jaxpr/all_gather | solution.py:52
  131.0 0.9 fusion.69
  131.9 0.3 dynamic-update-slice.2
  132.2 3.8 %all-reduce.2 = bf16[128]{0:T(256)(128)(2,1)S(1)} all-reduce(bf16[128]{0:T(256)(128)(2,1)S(1)} %dynamic-update-slice.2), channel_id=1, replica_groups=mesh['dp'=2,'expert'=16] {'dp'}, use_global_device_ids=true, to_apply=%add | all-reduce | flops 128 | bytes 512 | tf_op jit(solution)/shard_map/while
  136.0 0.7 copy.61
  136.7 3.2 %all-to-all-start.3 = ((bf16[2,16,4]{1,2,0:T(4,128)(2,1)}), bf16[2,16,4]{1,2,0:T(4,128)(2,1)S(1)}, u32[]{:S(2)}, u32[]{:S(2)}) async-start(bf16[2,16,4]{1,2,0:T(4,128)(2,1)} %copy.61), calls=%async_computation.3 | async-start | bytes 4096 | tf_op jit(solution)/shard_map/while/body/eval_jaxpr/all_to_all | solution.py:72
  140.0 8.2 %fusion.68 = bf16[128,2880]{0,1:T(8,128)(2,1)S(1)} fusion(bf16[2,1,720,2880]{3,2,1,0:T(8,128)(2,1)} %get-tuple-element.130, s32[]{:T(128)} %get-tuple-element.112, bf16[128,2880]{1,0:T(8,128)(2,1)S(1)} %all_gather.7, bf16[2,1,2880,720]{2,3,1,0:T(8,128)(2,1)} %get-tuple-element.129), kind=kOutput, calls=%fused_computation.6.clone.1 | convolution fusion | flops 1062512640 | bytes 9954304 | tf_op jit(solution)/shard_map/while/body/eval_jaxpr/dot_general | solution.py:58
  148.2 0.4 copy.59
  148.5 1.1 reshape.106
  149.6 3.5 %all-to-all-start.1 = ((bf16[2,16,4,2880]{3,2,1,0:T(4,128)(2,1)}), bf16[2,16,4,2880]{3,2,1,0:T(4,128)(2,1)S(1)}, u32[]{:S(2)}, u32[]{:S(2)}) async-start(bf16[2,16,4,2880]{3,2,1,0:T(4,128)(2,1)} %reshape.106), calls=%async_computation.1 | async-start | bytes 1507328 | tf_op jit(solution)/shard_map/while/body/eval_jaxpr/all_to_all | solution.py:65
  153.1 0.7 copy.62
  153.8 7.4 %all-to-all-done.1 = bf16[2,16,4,2880]{3,2,1,0:T(4,128)(2,1)S(1)} async-done(((bf16[2,16,4,2880]{3,2,1,0:T(4,128)(2,1)}), bf16[2,16,4,2880]{3,2,1,0:T(4,128)(2,1)S(1)}, u32[]{:S(2)}, u32[]{:S(2)}) %all-to-all-start.1) | async-done | bytes 737312 | tf_op jit(solution)/shard_map/while/body/eval_jaxpr/all_to_all | solution.py:65
  161.2 7.1 %all-to-all-start.4 = ((bf16[2,16,4]{2,0,1:T(2,128)(2,1)}), bf16[2,16,4]{2,0,1:T(2,128)(2,1)S(1)}, u32[]{:S(2)}, u32[]{:S(2)}) async-start(bf16[2,16,4]{2,0,1:T(2,128)(2,1)} %copy.62), calls=%async_computation.4 | async-start | bytes 16384 | tf_op jit(solution)/shard_map/while/body/eval_jaxpr/all_to_all | solution.py:71
  168.3 1.1 copy.60
  169.5 4.6 %all-to-all-done.4 = bf16[2,16,4]{2,0,1:T(2,128)(2,1)S(1)} async-done(((bf16[2,16,4]{2,0,1:T(2,128)(2,1)}), bf16[2,16,4]{2,0,1:T(2,128)(2,1)S(1)}, u32[]{:S(2)}, u32[]{:S(2)}) %all-to-all-start.4) | async-done | bytes 288 | tf_op jit(solution)/shard_map/while/body/eval_jaxpr/all_to_all | solution.py:71
  174.1 4.1 %all-to-all-start.2 = ((bf16[2,16,4,2880]{3,2,0,1:T(4,128)(2,1)}), bf16[2,16,4,2880]{3,2,0,1:T(4,128)(2,1)S(1)}, u32[]{:S(2)}, u32[]{:S(2)}) async-start(bf16[2,16,4,2880]{3,2,0,1:T(4,128)(2,1)} %copy.60), calls=%async_computation.2 | async-start | bytes 1507328 | tf_op jit(solution)/shard_map/while/body/eval_jaxpr/all_to_all | solution.py:64
  178.3 0.1 multiply_reduce_fusion.2
  178.4 17.9 %all-to-all-done.2 = bf16[2,16,4,2880]{3,2,0,1:T(4,128)(2,1)S(1)} async-done(((bf16[2,16,4,2880]{3,2,0,1:T(4,128)(2,1)}), bf16[2,16,4,2880]{3,2,0,1:T(4,128)(2,1)S(1)}, u32[]{:S(2)}, u32[]{:S(2)}) %all-to-all-start.2) | async-done | bytes 737312 | tf_op jit(solution)/shard_map/while/body/eval_jaxpr/all_to_all | solution.py:64
  196.4 0.3 fusion.70
  196.7 0.6 copy-done
  (30 shorter events, 1.5 us)
Async XLA Ops:
  4.4 18.9 %all-to-all-start = ((bf16[16,4,2880]{2,1,0:T(4,128)(2,1)}), bf16[16,4,2880]{2,1,0:T(4,128)(2,1)S(1)}, u32[]{:S(2)}, u32[]{:S(2)}) async-start(bf16[16,4,2880]{2,1,0:T(4,128)(2,1)} %copy.58), calls=%async_computation | async-start | bytes 753664 | tf_op jit(solution)/shard_map/while/body/eval_jaxpr/all_to_all | solution.py:45
  39.8 12.9 %all-to-all-start.3 = ((bf16[2,16,4]{1,2,0:T(4,128)(2,1)}), bf16[2,16,4]{1,2,0:T(4,128)(2,1)S(1)}, u32[]{:S(2)}, u32[]{:S(2)}) async-start(bf16[2,16,4]{1,2,0:T(4,128)(2,1)} %copy.61), calls=%async_computation.3 | async-start | bytes 4096 | tf_op jit(solution)/shard_map/while/body/eval_jaxpr/all_to_all | solution.py:72
  52.7 11.6 %all-to-all-start.1 = ((bf16[2,16,4,2880]{3,2,1,0:T(4,128)(2,1)}), bf16[2,16,4,2880]{3,2,1,0:T(4,128)(2,1)S(1)}, u32[]{:S(2)}, u32[]{:S(2)}) async-start(bf16[2,16,4,2880]{3,2,1,0:T(4,128)(2,1)} %reshape.106), calls=%async_computation.1 | async-start | bytes 1507328 | tf_op jit(solution)/shard_map/while/body/eval_jaxpr/all_to_all | solution.py:65
  64.3 12.8 %all-to-all-start.4 = ((bf16[2,16,4]{2,0,1:T(2,128)(2,1)}), bf16[2,16,4]{2,0,1:T(2,128)(2,1)S(1)}, u32[]{:S(2)}, u32[]{:S(2)}) async-start(bf16[2,16,4]{2,0,1:T(2,128)(2,1)} %copy.62), calls=%async_computation.4 | async-start | bytes 16384 | tf_op jit(solution)/shard_map/while/body/eval_jaxpr/all_to_all | solution.py:71
  77.1 22.2 %all-to-all-start.2 = ((bf16[2,16,4,2880]{3,2,0,1:T(4,128)(2,1)}), bf16[2,16,4,2880]{3,2,0,1:T(4,128)(2,1)S(1)}, u32[]{:S(2)}, u32[]{:S(2)}) async-start(bf16[2,16,4,2880]{3,2,0,1:T(4,128)(2,1)} %copy.60), calls=%async_computation.2 | async-start | bytes 1507328 | tf_op jit(solution)/shard_map/while/body/eval_jaxpr/all_to_all | solution.py:64
  103.4 16.9 %all-to-all-start = ((bf16[16,4,2880]{2,1,0:T(4,128)(2,1)}), bf16[16,4,2880]{2,1,0:T(4,128)(2,1)S(1)}, u32[]{:S(2)}, u32[]{:S(2)}) async-start(bf16[16,4,2880]{2,1,0:T(4,128)(2,1)} %copy.58), calls=%async_computation | async-start | bytes 753664 | tf_op jit(solution)/shard_map/while/body/eval_jaxpr/all_to_all | solution.py:45
  136.7 12.9 %all-to-all-start.3 = ((bf16[2,16,4]{1,2,0:T(4,128)(2,1)}), bf16[2,16,4]{1,2,0:T(4,128)(2,1)S(1)}, u32[]{:S(2)}, u32[]{:S(2)}) async-start(bf16[2,16,4]{1,2,0:T(4,128)(2,1)} %copy.61), calls=%async_computation.3 | async-start | bytes 4096 | tf_op jit(solution)/shard_map/while/body/eval_jaxpr/all_to_all | solution.py:72
  149.6 11.6 %all-to-all-start.1 = ((bf16[2,16,4,2880]{3,2,1,0:T(4,128)(2,1)}), bf16[2,16,4,2880]{3,2,1,0:T(4,128)(2,1)S(1)}, u32[]{:S(2)}, u32[]{:S(2)}) async-start(bf16[2,16,4,2880]{3,2,1,0:T(4,128)(2,1)} %reshape.106), calls=%async_computation.1 | async-start | bytes 1507328 | tf_op jit(solution)/shard_map/while/body/eval_jaxpr/all_to_all | solution.py:65
  161.2 12.8 %all-to-all-start.4 = ((bf16[2,16,4]{2,0,1:T(2,128)(2,1)}), bf16[2,16,4]{2,0,1:T(2,128)(2,1)S(1)}, u32[]{:S(2)}, u32[]{:S(2)}) async-start(bf16[2,16,4]{2,0,1:T(2,128)(2,1)} %copy.62), calls=%async_computation.4 | async-start | bytes 16384 | tf_op jit(solution)/shard_map/while/body/eval_jaxpr/all_to_all | solution.py:71
  174.1 22.2 %all-to-all-start.2 = ((bf16[2,16,4,2880]{3,2,0,1:T(4,128)(2,1)}), bf16[2,16,4,2880]{3,2,0,1:T(4,128)(2,1)S(1)}, u32[]{:S(2)}, u32[]{:S(2)}) async-start(bf16[2,16,4,2880]{3,2,0,1:T(4,128)(2,1)} %copy.60), calls=%async_computation.2 | async-start | bytes 1507328 | tf_op jit(solution)/shard_map/while/body/eval_jaxpr/all_to_all | solution.py:64
  196.7 0.6 copy-start
where the time goes:
time: 199 us; the launch traced here: 197 us
  waiting for transfers between devices  79.1 us (40%)
  starting transfers between devices  48.5 us (24%)
  blocking collectives  28.7 us (14%)
  matrix products  19.4 us (10%)
  local copies, waits for them, and re-layouts  18.1 us (9%)
    all_to_all x2, waiting for transfers between devices, layer_step(): lax.all_to_all(lax.all_to_all(part_sums, 'dp', split_axis=0, concat_axis=...  35.7 us
    all_gather x2, blocking collectives, layer_step(): lax.all_gather(arrived, 'dp', axis=0, tiled=True)  21.2 us
    all_to_all x2, waiting for transfers between devices, layer_step(): lax.all_to_all(outgoing, 'expert', split_axis=0, concat_axis=0, tiled=True)  19.4 us
    dot_general x2, matrix products, layer_step(): jnp.dot(hidden, down_part[0], preferred_element_type=jnp.float32)  16.4 us
    all_to_all x2, waiting for transfers between devices, layer_step(): lax.all_to_all(part_sums, 'dp', split_axis=0, concat_axis=0, tiled=True)  14.8 us
    all_to_all x2, starting transfers between devices, layer_step(): lax.all_to_all(lax.all_to_all(all_gates, 'dp', split_axis=0, concat_axis=...  14.2 us
    all_to_all x2, starting transfers between devices, layer_step(): lax.all_to_all(outgoing, 'expert', split_axis=0, concat_axis=0, tiled=True)  12.6 us
    all_to_all x2, waiting for transfers between devices, layer_step(): lax.all_to_all(lax.all_to_all(all_gates, 'dp', split_axis=0, concat_axis=...  9.21 us
  transfers between devices with their start and end apart: 10, of which 8 were waited for; matrix products, arithmetic and copies ran while one was open for 13% of the time, Pallas kernels for 0%

commit v1 on v0

--- a/solution.py
+++ b/solution.py
@@ -1,6 +1,10 @@
+import functools
+
 import jax
 import jax.numpy as jnp
 from jax import lax
+from jax.experimental import pallas as pl
+from jax.experimental.pallas import tpu as pltpu
 from jax.sharding import PartitionSpec as P
 
 
@@ -28,7 +32,7 @@
     return jnp.transpose(slot_map, (1, 2, 0))
 
 
-def per_device(tokens, routes, placement, up_weight, down_weight, router_weight):
+def plan_by_collectives(tokens, routes, placement, up_weight, down_weight, router_weight):
     groups = lax.axis_size("dp")
     columns = lax.axis_size("expert")
     tok_rows = tokens.shape[0]
@@ -93,6 +97,325 @@
     return result_stream
 
 
+LANES = 128
+PARTS = 4
+MESH = pl.DeviceIdType.MESH
+
+
+def fused_layers(
+    dims, init_ref, aux_ref, up_hbm, down_hbm, down_tail, out_ref,
+    pair, masks, stream, wide, shares, rows_in, up_v, down_v, acc, kept,
+    core_out, core_in, sums, in_a, mid, in_b, last, in_z, full,
+    w_sem, first_send, first_recv, send_sem, recv_sem,
+):
+    layers, depth, ny, nz, width, tok = dims
+    cols = width // (2 * PARTS)
+    main = depth // LANES * LANES
+    half_rows = 2 * tok
+    count = ny * nz * 2 * half_rows
+    whole_chunks = main // cols
+    y, e = lax.axis_index("dp"), lax.axis_index("expert")
+    core, x, z = e % 2, (e // 2) % 2, e // 4
+    home = core * PARTS
+    away = (1 - core) * PARTS
+
+    def device(y_to, z_to, x_to, core_to):
+        return (y_to, (z_to * 2 + x_to) * 2 + core_to)
+
+    weight_copies = []
+    for l in range(layers):
+        copies = [pltpu.make_async_copy(up_hbm.at[l, 0], up_v.at[l, pl.ds(0, depth)], w_sem.at[l, 0])]
+        for k in range(whole_chunks):
+            copies.append(pltpu.make_async_copy(
+                down_hbm.at[l, 0, :, pl.ds(k * cols, cols)], down_v.at[l, k], w_sem.at[l, 1 + k]))
+        rest = main - whole_chunks * cols
+        if rest:
+            copies.append(pltpu.make_async_copy(
+                down_hbm.at[l, 0, :, pl.ds(whole_chunks * cols, rest)],
+                down_v.at[l, whole_chunks, :, pl.ds(0, rest)], w_sem.at[l, 1 + whole_chunks]))
+        copies.append(pltpu.make_async_copy(
+            down_tail.at[l], down_v.at[l, whole_chunks, :, pl.ds(rest, width - main)], w_sem.at[l, 2 + whole_chunks]))
+        for copy in copies:
+            copy.start()
+        weight_copies.append(copies)
+
+    peers = [device(y, z, x, 1 - core), device(y, z, 1 - x, core)]
+    peers += [device((y + o) % ny, z, x, core) for o in range(1, ny)]
+    peers += [device(y, (z + o) % nz, x, core) for o in range(1, nz)]
+    barrier = pltpu.get_barrier_semaphore()
+    for peer in peers:
+        pl.semaphore_signal(barrier, inc=1, device_id=peer, device_id_type=MESH)
+    pl.semaphore_wait(barrier, len(peers))
+
+    first = pltpu.make_async_remote_copy(
+        src_ref=init_ref, dst_ref=pair, send_sem=first_send, recv_sem=first_recv,
+        device_id=device(y, z, x, 1 - core), device_id_type=MESH)
+    first.start()
+    for l in range(layers):
+        up_v[l, depth:width, :] = jnp.zeros((width - depth, up_v.shape[2]), jnp.bfloat16)
+    first.wait()
+    mine, other = init_ref[...].astype(jnp.float32), pair[...].astype(jnp.float32)
+    both = jnp.concatenate(
+        [jnp.where(core == 0, mine, other), jnp.where(core == 0, other, mine)], axis=0)
+    stream[...] = both[:, :width]
+    for l in range(layers):
+        start = width + l * (width - main)
+        masks[l] = both[:, start:start + width - main]
+
+    lane = lax.broadcasted_iota(jnp.int32, (half_rows, width), 1)
+    for l in range(layers):
+        pending = []
+        slot = [0]
+
+        def send(src, dst, peer):
+            n = slot[0]
+            slot[0] = n + 1
+            copy = pltpu.make_async_remote_copy(
+                src_ref=src, dst_ref=dst, send_sem=send_sem.at[l, n], recv_sem=recv_sem.at[l, n],
+                device_id=peer, device_id_type=MESH)
+            copy.start()
+            pending.append(copy)
+            return copy
+
+        def arrived(copies):
+            for copy in copies:
+                copy.wait_recv()
+
+        values = stream[...]
+        inverse = lax.rsqrt(jnp.sum(values * values, axis=-1, keepdims=True) / depth + 1e-05)
+        wide[...] = values * inverse
+        wide[:, main:width] += masks[l]
+        for k in range(2 * PARTS):
+            shares[l, k] = wide[:, k * cols:(k + 1) * cols].astype(jnp.bfloat16)
+
+        step = []
+        for j in range(PARTS):
+            k = home + j
+            step.append([
+                send(shares.at[l, k], rows_in.at[l, k, y, z, x], device(y, (z + o) % nz, x, core))
+                for o in range(1, nz)])
+        for j in range(PARTS):
+            rows_in[l, home + j, y, z, x] = shares[l, home + j]
+        next_step = []
+        for j in range(PARTS):
+            k = home + j
+            arrived(step[j])
+            if j % 2 == 0:
+                next_step.append([send(rows_in.at[l, k, y, :, x], rows_in.at[l, k, y, :, x], device(y, z, 1 - x, core))])
+            else:
+                next_step.append([
+                    send(rows_in.at[l, k, y, :, x], rows_in.at[l, k, y, :, x], device((y + o) % ny, z, x, core))
+                    for o in range(1, ny)])
+        step, next_step = next_step, []
+        for j in range(PARTS):
+            k = home + j
+            arrived(step[j])
+            if j % 2 == 0:
+                next_step.append([
+                    send(rows_in.at[l, k, y], rows_in.at[l, k, y], device((y + o) % ny, z, x, core))
+                    for o in range(1, ny)])
+            else:
+                next_step.append([send(rows_in.at[l, k, :, :, x], rows_in.at[l, k, :, :, x], device(y, z, 1 - x, core))])
+        step, next_step = next_step, []
+        weight_copies[l][0].wait()
+
+        def multiply(k, opening):
+            block = rows_in[l, k].reshape(count, cols)
+            grown = jnp.dot(block, up_v[l, pl.ds(pl.multiple_of(k * cols, cols), cols), :], preferred_element_type=jnp.float32)
+            gates = lax.dot_general(block, aux_ref[l, k], (((1,), (1,)), ((), ())), preferred_element_type=jnp.float32)
+            if opening:
+                acc[...] = grown
+                kept[...] = gates
+            else:
+                acc[...] += grown
+                kept[...] += gates
+
+        for j in range(PARTS):
+            arrived(step[j])
+            next_step.append([send(rows_in.at[l, home + j], rows_in.at[l, home + j], device(y, z, x, 1 - core))])
+            multiply(home + j, j == 0)
+        step = next_step
+        for j in range(PARTS):
+            arrived(step[j])
+            multiply(away + j, False)
+
+        before = acc[...]
+        hidden = (before / (1.0 + jnp.exp(-before))).astype(jnp.bfloat16)
+        affinity = jax.nn.sigmoid(kept[:, 0:1]).astype(jnp.bfloat16).astype(jnp.float32)
+        gate = affinity * kept[:, 1:2]
+        counts_once = jnp.where(y == 0, 1.0, 0.0)
+        for copy in weight_copies[l][1:]:
+            copy.wait()
+
+        def outcome(k):
+            part = jnp.dot(hidden, down_v[l, k], preferred_element_type=jnp.float32)
+            marker = aux_ref[l, k].astype(jnp.float32)[1:2] * counts_once
+            return gate * (part + marker)
+
+        step, next_step = [], []
+        for j in range(PARTS):
+            core_out[l, j] = outcome(away + j).astype(jnp.bfloat16)
+            step.append([send(core_out.at[l, j], core_in.at[l, j], device(y, z, x, 1 - core))])
+        for j in range(PARTS):
+            own = outcome(home + j)
+            arrived(step[j])
+            total = (own + core_in[l, j].astype(jnp.float32)).astype(jnp.bfloat16)
+            sums[l, j] = total.reshape(ny, nz, 2, half_rows, cols)
+            if j % 2 == 0:
+                next_step.append([
+                    send(sums.at[l, j, (y + o) % ny], in_a[0].at[l, j // 2, o - 1], device((y + o) % ny, z, x, core))
+                    for o in range(1, ny)])
+            else:
+                next_step.append([send(sums.at[l, j, :, :, 1 - x], in_a[1].at[l, j // 2], device(y, z, 1 - x, core))])
+        step, next_step = next_step, []
+        for j in range(PARTS):
+            arrived(step[j])
+            i = j // 2
+            if j % 2 == 0:
+                total = sums[l, j, y].astype(jnp.float32)
+                for o in range(1, ny):
+                    total += in_a[0][l, i, o - 1].astype(jnp.float32)
+                mid[0][l, i] = total.astype(jnp.bfloat16)
+                next_step.append([send(mid[0].at[l, i, :, 1 - x], in_b.at[l, j, 0], device(y, z, 1 - x, core))])
+            else:
+                total = sums[l, j, :, :, x].astype(jnp.float32) + in_a[1][l, i].astype(jnp.float32)
+                mid[1][l, i] = total.astype(jnp.bfloat16)
+                next_step.append([
+                    send(mid[1].at[l, i, (y + o) % ny], in_b.at[l, j, o - 1], device((y + o) % ny, z, x, core))
+                    for o in range(1, ny)])
+        step, next_step = next_step, []
+        for j in range(PARTS):
+            arrived(step[j])
+            i = j // 2
+            if j % 2 == 0:
+                total = mid[0][l, i, :, x].astype(jnp.float32) + in_b[l, j, 0].astype(jnp.float32)
+            else:
+                total = mid[1][l, i, y].astype(jnp.float32)
+                for o in range(1, ny):
+                    total += in_b[l, j, o - 1].astype(jnp.float32)
+            last[l, j] = total.astype(jnp.bfloat16)
+            next_step.append([
+                send(last.at[l, j, (z + o) % nz], in_z.at[l, j, o - 1], device(y, (z + o) % nz, x, core))
+                for o in range(1, nz)])
+        step = next_step
+        for j in range(PARTS):
+            arrived(step[j])
+            total = last[l, j, z].astype(jnp.float32)
+            for o in range(1, nz):
+                total += in_z[l, j, o - 1].astype(jnp.float32)
+            full[l, home + j] = total.astype(jnp.bfloat16)
+        arrived([send(full.at[l, pl.ds(home, PARTS)], full.at[l, pl.ds(home, PARTS)], device(y, z, x, 1 - core))])
+        for k in range(2 * PARTS):
+            wide[:, k * cols:(k + 1) * cols] = full[l, k].astype(jnp.float32)
+        raw = wide[...]
+        denominator = jnp.sum(jnp.where(lane < depth, 0.0, raw), axis=-1, keepdims=True)
+        updated = stream[...] + jnp.where(lane < depth, raw, 0.0) / jnp.maximum(denominator, 0.5)
+        stream[...] = updated.astype(jnp.bfloat16).astype(jnp.float32)
+        for copy in pending:
+            copy.wait_send()
+    result = jnp.where(core == 0, stream[0:tok, :depth], stream[tok:half_rows, :depth])
+    out_ref[...] = result.astype(jnp.bfloat16)
+
+
+def plan_by_kernel(tokens, routes, placement, up_weight, down_weight, router_weight):
+    ny, columns = lax.axis_size("dp"), lax.axis_size("expert")
+    nz = columns // 4
+    tok, depth = tokens.shape
+    layers, experts = placement.shape
+    block = up_weight.shape[3]
+    width = padded_width(depth, experts)
+    cols = width // (2 * PARTS)
+    main = depth // LANES * LANES
+    half_rows = 2 * tok
+    count = ny * columns * tok
+    slots = jnp.arange(experts, dtype=jnp.int32)
+    place_of = jnp.sum(
+        jnp.where(routes[..., None] == slots, placement[:, None, None, :], 0), axis=3)
+    routed = jnp.any(place_of[..., None] == slots, axis=2).astype(jnp.bfloat16)
+    marks = jnp.pad(routed, ((0, 0), (0, 0), (depth - main, width - depth - experts)))
+    init = jnp.concatenate(
+        [jnp.pad(tokens, ((0, 0), (0, width - depth)))] + [marks[l] for l in range(layers)], axis=1)
+    router_row = jnp.pad(router_weight[:, 0], ((0, 0), (0, width - depth)))
+    own = (jnp.arange(width, dtype=jnp.int32) == depth + lax.axis_index("expert")).astype(jnp.bfloat16)
+    aux = jnp.stack([router_row, jnp.broadcast_to(own, router_row.shape)], axis=1)
+    aux = jnp.pad(aux, ((0, 0), (0, 14), (0, 0)))
+    aux = jnp.transpose(aux.reshape(layers, 16, 2 * PARTS, cols), (0, 2, 1, 3))
+    down_tail = jnp.pad(down_weight[:, 0, :, main:], ((0, 0), (0, 0), (0, width - depth)))
+    sends = PARTS * (2 * (nz - 1) + 2 * ny + 2) + 1
+    bf16, f32 = jnp.bfloat16, jnp.float32
+    in_vmem, anywhere = pl.BlockSpec(memory_space=pltpu.VMEM), pl.BlockSpec(memory_space=pl.ANY)
+    return pl.pallas_call(
+        functools.partial(fused_layers, (layers, depth, ny, nz, width, tok)),
+        out_shape=jax.ShapeDtypeStruct((tok, depth), bf16),
+        in_specs=[in_vmem, in_vmem, anywhere, anywhere, anywhere],
+        out_specs=in_vmem,
+        scratch_shapes=[
+            pltpu.VMEM(init.shape, bf16),
+            pltpu.VMEM((layers, half_rows, width - main), f32),
+            pltpu.VMEM((half_rows, width), f32),
+            pltpu.VMEM((half_rows, width), f32),
+            pltpu.VMEM((layers, 2 * PARTS, half_rows, cols), bf16),
+            pltpu.VMEM((layers, 2 * PARTS, ny, nz, 2, half_rows, cols), bf16),
+            pltpu.VMEM((layers, width, block), bf16),
+            pltpu.VMEM((layers, 2 * PARTS, block, cols), bf16),
+            pltpu.VMEM((count, block), f32),
+            pltpu.VMEM((count, 16), f32),
+            pltpu.VMEM((layers, PARTS, count, cols), bf16),
+            pltpu.VMEM((layers, PARTS, count, cols), bf16),
+            pltpu.VMEM((layers, PARTS, ny, nz, 2, half_rows, cols), bf16),
+            [
+                pltpu.VMEM((layers, PARTS // 2, ny - 1, nz, 2, half_rows, cols), bf16),
+                pltpu.VMEM((layers, PARTS // 2, ny, nz, half_rows, cols), bf16),
+            ],
+            [
+                pltpu.VMEM((layers, PARTS // 2, nz, 2, half_rows, cols), bf16),
+                pltpu.VMEM((layers, PARTS // 2, ny, nz, half_rows, cols), bf16),
+            ],
+            pltpu.VMEM((layers, PARTS, ny - 1, nz, half_rows, cols), bf16),
+            pltpu.VMEM((layers, PARTS, nz, half_rows, cols), bf16),
+            pltpu.VMEM((layers, PARTS, nz - 1, half_rows, cols), bf16),
+            pltpu.VMEM((layers, 2 * PARTS, half_rows, cols), bf16),
+            pltpu.SemaphoreType.DMA((layers, 3 + main // cols)),
+            pltpu.SemaphoreType.DMA,
+            pltpu.SemaphoreType.DMA,
+            pltpu.SemaphoreType.DMA((layers, sends)),
+            pltpu.SemaphoreType.DMA((layers, sends)),
+        ],
+        compiler_params=pltpu.CompilerParams(
+            collective_id=0, has_side_effects=True, vmem_limit_bytes=VMEM_BYTES),
+    )(init, aux, up_weight, down_weight, down_tail)
+
+
+VMEM_BYTES = 60 << 20
+
+
+def padded_width(depth, experts):
+    unit = 2 * PARTS * LANES
+    return -(-(depth + experts) // unit) * unit
+
+
+def kernel_fits(ny, columns, tokens, placement, up_weight):
+    tok, depth = tokens.shape
+    layers, experts = placement.shape
+    block = up_weight.shape[3]
+    width = padded_width(depth, experts)
+    main = depth // LANES * LANES
+    count = ny * columns * tok
+    lanes = -(-block // LANES) * LANES
+    need = layers * 2 * width * (2 * lanes + 4 * count) + 4 * count * (3 * lanes + width // 4)
+    return (
+        ny > 1 and columns % 4 == 0 and columns > 4 and experts == columns and up_weight.shape[1] == 1
+        and tok % 8 == 0 and depth % 16 == 0 and block % 16 == 0
+        and width - main <= width // (2 * PARTS) and need < VMEM_BYTES
+    )
+
+
+def per_device(tokens, routes, placement, up_weight, down_weight, router_weight):
+    fits = kernel_fits(lax.axis_size("dp"), lax.axis_size("expert"), tokens, placement, up_weight)
+    plan = plan_by_kernel if fits else plan_by_collectives
+    return plan(tokens, routes, placement, up_weight, down_weight, router_weight)
+
+
 def solution(mesh):
     return jax.shard_map(
         per_device,

time: 199 us -> 96.3 us (0.48)
  waiting for transfers between devices: 79.1 us -> 0 us
  Pallas kernels: 0 us -> 76.1 us
  starting transfers between devices: 48.5 us -> 0 us
  blocking collectives: 28.7 us -> 0 us
  matrix products: 19.4 us -> 0 us
    all_to_all x10 -> x0, waiting for transfers between devices: 79.1 us -> none  [the longest x2 35.7 us: layer_step(): lax.all_to_all(lax.all_to_all(part_sums, 'dp', split_axis=0, concat_axis=...]
    pallas_call x0 -> x1, Pallas kernels: none -> 76.1 us  [plan_by_kernel(): pl.pallas_call(functools.partial(fused_layers, (layers, depth, ny, nz, wi...]
    all_to_all x10 -> x0, starting transfers between devices: 48.5 us -> none  [the longest x2 14.2 us: layer_step(): lax.all_to_all(lax.all_to_all(all_gates, 'dp', split_axis=0, concat_axis=...]
    all_gather x2 -> x0, blocking collectives: 21.2 us -> none  [layer_step(): lax.all_gather(arrived, 'dp', axis=0, tiled=True)]
    dot_general x8 -> x0, matrix products: 19.4 us -> none  [the longest x2 16.4 us: layer_step(): jnp.dot(hidden, down_part[0], preferred_element_type=jnp.float32)]
    unnamed x3 -> x2, local copies, waits for them, and re-layouts: 1.41 us -> 13.2 us
    while x2 -> x0, blocking collectives: 7.51 us -> none
    all_to_all x4 -> x0, local copies, waits for them, and re-layouts: 3.67 us -> none  [the longest x2 2.26 us: layer_step(): lax.all_to_all(part_sums, 'dp', split_axis=0, concat_axis=0, tiled=True)]
  transfers between devices with their start and end apart: 10 -> 0, of which waited for: 8 -> 0; matrix products, arithmetic and copies ran while one was open for 13% -> 0% of each run, Pallas kernels for 0% -> 0%
where the time goes in v1:
time: 96.3 us; the launch traced here: 95.7 us
  Pallas kernels  76.1 us (79%)
  local copies, waits for them, and re-layouts  16.8 us (17%)
  other arithmetic  2.68 us (3%)
    pallas_call x1, Pallas kernels, plan_by_kernel(): pl.pallas_call(functools.partial(fused_layers, (layers, depth, ny, nz, wi...  76.1 us
    unnamed x2, local copies, waits for them, and re-layouts  13.2 us

profile of v1, /device:TPU:1, one launch (start us, length us, event | category | flops | bytes accessed | tf_op | source)
XLA Modules:
  0.0 95.7 jit_solution(6522234256129734070)
XLA Ops:
  0.0 1.0 %select_reduce_fusion = s32[2,8,4]{1,2,0:T(4,128)S(1)} fusion(s32[2,16]{1,0:T(2,128)} %param.8, s32[2,8,4]{1,2,0:T(4,128)} %param.7), kind=kLoop, calls=%fused_computation.11 | loop fusion | flops 3008 | bytes 640 | tf_op jit(solution)/shard_map/reduce_sum | solution.py:332
  1.0 0.1 fusion.6
  1.1 0.1 pad_convert_fusion
  1.2 0.7 pad_bitcast_fusion
  1.9 1.4 %fusion.5.init_ref = bf16[8,3584]{1,0:T(8,128)(2,1)} fusion(bf16[8,2880]{1,0:T(8,128)(2,1)} %param.6, bf16[8,256]{1,0:T(8,128)(2,1)S(1)} %get-tuple-element.6, bf16[8,256]{1,0:T(8,128)(2,1)S(1)} %get-tuple-element.5), kind=kLoop, calls=%fused_computation.9 | loop fusion | flops 229376 | bytes 111616 | tf_op jit(solution)/shard_map/concatenate | solution.py:336
  3.3 0.1 fusion.2
  3.5 0.1 reshape.7
  3.6 0.7 copy.22
  4.3 1.0 %slice_bitcast_fusion = bf16[2,720,64]{2,1,0:T(8,128)(2,1)S(1)} fusion(bf16[2,1,720,2880]{3,2,0,1:T(8,128)(2,1)} %bitcast.15), kind=kLoop, calls=%fused_computation.3 | loop fusion | bytes 368640 | tf_op jit(solution)/shard_map/squeeze | solution.py:343
  5.3 1.1 %pad.28.down_tail = bf16[2,720,256]{2,1,0:T(8,128)(2,1)} pad(bf16[2,720,64]{2,1,0:T(8,128)(2,1)S(1)} %slice_bitcast_fusion, bf16[]{:T(256)} %constant.3.clone.1), padding=0_0x0_0x0_192 | pad | bytes 921602 | tf_op jit(solution)/shard_map/jit(_pad)/pad | solution.py:343
  6.4 11.8 %copy.18.up_hbm = bf16[2,1,2880,720]{3,2,1,0:T(8,128)(2,1)} copy(bf16[2,1,2880,720]{2,3,1,0:T(8,128)(2,1)} %param.9) | data formatting | bytes 16588800 | tf_op args[3]
  18.1 76.1 %shard_map.64 = bf16[8,2880]{1,0:T(8,128)(2,1)} custom-call(bf16[8,3584]{1,0:T(8,128)(2,1)} %fusion.5.init_ref, bf16[2,8,16,384]{3,2,1,0:T(8,128)(2,1)} %bitcast.16, bf16[2,1,2880,720]{3,2,1,0:T(8,128)(2,1)} %copy.18.up_hbm, bf16[2,1,720,2880]{3,2,1,0:T(8,128)(2,1)} %down_hbm.1, bf16[2,720,256]{2,1,0:T(8,128)(2,1)} %pad.28.down_tail), custom_call_target="tpu_custom_call" | custom-call | tf_op jit(solution)/shard_map/pallas_call | solution.py:347
  94.3 1.4 %copy.24 = bf16[8,2880]{1,0:T(8,128)(2,1)} copy(bf16[8,2880]{1,0:T(8,128)(2,1)} %shard_map.64) | data formatting | bytes 92160
  (3 shorter events, 0.0 us)

commit v2 on v1

--- a/solution.py
+++ b/solution.py
@@ -99,42 +99,36 @@
 
 LANES = 128
 PARTS = 4
+ORDERS = ("zxy", "zyx", "xzy", "yzx")
+SECOND, THIRD = (2, 3, 0, 1), (0, 1, 2, 3)
 MESH = pl.DeviceIdType.MESH
 
 
 def fused_layers(
-    dims, init_ref, aux_ref, up_hbm, down_hbm, down_tail, out_ref,
-    pair, masks, stream, wide, shares, rows_in, up_v, down_v, acc, kept,
+    dims, tokens_ref, routes_ref, placement_ref, router_ref, up_hbm, down_hbm, out_ref,
+    marks, pair, pair_marks, aux_ref, tail_up, tail_down, masks, stream, wide, shares, rows_in, up_v, down_v, acc, kept,
     core_out, core_in, sums, in_a, mid, in_b, last, in_z, full,
     w_sem, first_send, first_recv, send_sem, recv_sem,
 ):
-    layers, depth, ny, nz, width, tok = dims
+    layers, depth, ny, nz, width, tok, top_k, experts = dims
     cols = width // (2 * PARTS)
     main = depth // LANES * LANES
     half_rows = 2 * tok
     count = ny * nz * 2 * half_rows
-    whole_chunks = main // cols
+    edge = (2 * PARTS - 1) * cols
     y, e = lax.axis_index("dp"), lax.axis_index("expert")
     core, x, z = e % 2, (e // 2) % 2, e // 4
     home = core * PARTS
-    away = (1 - core) * PARTS
 
     def device(y_to, z_to, x_to, core_to):
         return (y_to, (z_to * 2 + x_to) * 2 + core_to)
 
     weight_copies = []
     for l in range(layers):
-        copies = [pltpu.make_async_copy(up_hbm.at[l, 0], up_v.at[l, pl.ds(0, depth)], w_sem.at[l, 0])]
-        for k in range(whole_chunks):
-            copies.append(pltpu.make_async_copy(
-                down_hbm.at[l, 0, :, pl.ds(k * cols, cols)], down_v.at[l, k], w_sem.at[l, 1 + k]))
-        rest = main - whole_chunks * cols
-        if rest:
-            copies.append(pltpu.make_async_copy(
-                down_hbm.at[l, 0, :, pl.ds(whole_chunks * cols, rest)],
-                down_v.at[l, whole_chunks, :, pl.ds(0, rest)], w_sem.at[l, 1 + whole_chunks]))
-        copies.append(pltpu.make_async_copy(
-            down_tail.at[l], down_v.at[l, whole_chunks, :, pl.ds(rest, width - main)], w_sem.at[l, 2 + whole_chunks]))
+        copies = [
+            pltpu.make_async_copy(up_hbm.at[l, 0], up_v.at[l], w_sem.at[l, 0]),
+            pltpu.make_async_copy(down_hbm.at[l, 0], down_v.at[l], w_sem.at[l, 1]),
+        ]
         for copy in copies:
             copy.start()
         weight_copies.append(copies)
@@ -147,22 +141,55 @@
         pl.semaphore_signal(barrier, inc=1, device_id=peer, device_id_type=MESH)
     pl.semaphore_wait(barrier, len(peers))
 
+    partner = device(y, z, x, 1 - core)
     first = pltpu.make_async_remote_copy(
-        src_ref=init_ref, dst_ref=pair, send_sem=first_send, recv_sem=first_recv,
-        device_id=device(y, z, x, 1 - core), device_id_type=MESH)
+        src_ref=tokens_ref, dst_ref=pair, send_sem=first_send.at[0], recv_sem=first_recv.at[0],
+        device_id=partner, device_id_type=MESH)
     first.start()
+    expert_row = lax.broadcasted_iota(jnp.int32, (tok, experts), 1)
+    slot_row = lax.broadcasted_iota(jnp.int32, (width - main, experts), 0) - (depth - main)
     for l in range(layers):
-        up_v[l, depth:width, :] = jnp.zeros((width - depth, up_v.shape[2]), jnp.bfloat16)
+        hits = jnp.zeros((tok, experts), jnp.float32)
+        for k in range(top_k):
+            hits += jnp.where(routes_ref[l, :, k:k + 1] == expert_row, 1.0, 0.0)
+        served = jnp.where(placement_ref[l:l + 1, :] == slot_row, 1.0, 0.0)
+        marks[l] = lax.dot_general(
+            hits.astype(jnp.bfloat16), served.astype(jnp.bfloat16), (((1,), (1,)), ((), ())),
+            preferred_element_type=jnp.float32).astype(jnp.bfloat16)
+    second = pltpu.make_async_remote_copy(
+        src_ref=marks, dst_ref=pair_marks, send_sem=first_send.at[1], recv_sem=first_recv.at[1],
+        device_id=partner, device_id_type=MESH)
+    second.start()
+    lane = lax.broadcasted_iota(jnp.int32, (half_rows, width), 1)
+    row = lax.broadcasted_iota(jnp.int32, (half_rows, width), 0)
+    for l in range(layers):
+        wide[...] = jnp.where((row == 1) & (lane == depth + e), 1.0, 0.0)
+        wide[0:1, 0:depth] = router_ref[l:l + 1, :].astype(jnp.float32)
+        for k in range(2 * PARTS):
+            aux_ref[l, k] = wide[:, k * cols:(k + 1) * cols].astype(jnp.bfloat16)
+    stream[...] = jnp.zeros_like(stream)
+
+    def paired(mine, other):
+        mine, other = mine.astype(jnp.float32), other.astype(jnp.float32)
+        return jnp.concatenate(
+            [jnp.where(core == 0, mine, other), jnp.where(core == 0, other, mine)], axis=0)
+
     first.wait()
-    mine, other = init_ref[...].astype(jnp.float32), pair[...].astype(jnp.float32)
-    both = jnp.concatenate(
-        [jnp.where(core == 0, mine, other), jnp.where(core == 0, other, mine)], axis=0)
-    stream[...] = both[:, :width]
+    stream[:, 0:depth] = paired(tokens_ref[...], pair[...])
+    second.wait()
     for l in range(layers):
-        start = width + l * (width - main)
-        masks[l] = both[:, start:start + width - main]
-
-    lane = lax.broadcasted_iota(jnp.int32, (half_rows, width), 1)
+        masks[l] = paired(marks[l], pair_marks[l])
+
+    def fill_tail(tail, whole, l):
+        tail[l] = jnp.zeros(tail.shape[1:], jnp.bfloat16)
+        tail[l, :, 0:depth - edge] = whole[l, :, edge:depth]
+
+    def chunk(whole, tail, l, side, j):
+        if j < PARTS - 1:
+            return whole[l, :, pl.ds(pl.multiple_of((side * PARTS + j) * cols, cols), cols)]
+        early = whole[l, :, (PARTS - 1) * cols:PARTS * cols]
+        return jnp.where(side == 0, early, tail[l])
+
     for l in range(layers):
         pending = []
         slot = [0]
@@ -188,40 +215,37 @@
         for k in range(2 * PARTS):
             shares[l, k] = wide[:, k * cols:(k + 1) * cols].astype(jnp.bfloat16)
 
-        step = []
-        for j in range(PARTS):
+        def spread(j, done, axis):
             k = home + j
-            step.append([
-                send(shares.at[l, k], rows_in.at[l, k, y, z, x], device(y, (z + o) % nz, x, core))
-                for o in range(1, nz)])
+            at = (
+                slice(None) if "y" in done else y,
+                slice(None) if "z" in done else z,
+                slice(None) if "x" in done else x,
+            )
+            src = rows_in.at[(l, k) + at] if done else shares.at[l, k]
+            return [send(src, rows_in.at[(l, k) + at], peer) for peer in along[axis]]
+
+        along = {
+            "x": [device(y, z, 1 - x, core)],
+            "y": [device((y + o) % ny, z, x, core) for o in range(1, ny)],
+            "z": [device(y, (z + o) % nz, x, core) for o in range(1, nz)],
+        }
+        step = {j: spread(j, "", ORDERS[j][0]) for j in range(PARTS)}
         for j in range(PARTS):
             rows_in[l, home + j, y, z, x] = shares[l, home + j]
+        for s, turn in ((1, SECOND), (2, THIRD)):
+            for j in turn:
+                arrived(step[j])
+                step[j] = spread(j, ORDERS[j][:s], ORDERS[j][s])
         next_step = []
-        for j in range(PARTS):
-            k = home + j
-            arrived(step[j])
-            if j % 2 == 0:
-                next_step.append([send(rows_in.at[l, k, y, :, x], rows_in.at[l, k, y, :, x], device(y, z, 1 - x, core))])
-            else:
-                next_step.append([
-                    send(rows_in.at[l, k, y, :, x], rows_in.at[l, k, y, :, x], device((y + o) % ny, z, x, core))
-                    for o in range(1, ny)])
-        step, next_step = next_step, []
-        for j in range(PARTS):
-            k = home + j
-            arrived(step[j])
-            if j % 2 == 0:
-                next_step.append([
-                    send(rows_in.at[l, k, y], rows_in.at[l, k, y], device((y + o) % ny, z, x, core))
-                    for o in range(1, ny)])
-            else:
-                next_step.append([send(rows_in.at[l, k, :, :, x], rows_in.at[l, k, :, :, x], device(y, z, 1 - x, core))])
-        step, next_step = next_step, []
         weight_copies[l][0].wait()
-
-        def multiply(k, opening):
+        fill_tail(tail_up, up_v, l)
+
+        def multiply(side, j, opening):
+            k = side * PARTS + j
             block = rows_in[l, k].reshape(count, cols)
-            grown = jnp.dot(block, up_v[l, pl.ds(pl.multiple_of(k * cols, cols), cols), :], preferred_element_type=jnp.float32)
+            grown = lax.dot_general(
+                block, chunk(up_v, tail_up, l, side, j), (((1,), (1,)), ((), ())), preferred_element_type=jnp.float32)
             gates = lax.dot_general(block, aux_ref[l, k], (((1,), (1,)), ((), ())), preferred_element_type=jnp.float32)
             if opening:
                 acc[...] = grown
@@ -233,31 +257,32 @@
         for j in range(PARTS):
             arrived(step[j])
             next_step.append([send(rows_in.at[l, home + j], rows_in.at[l, home + j], device(y, z, x, 1 - core))])
-            multiply(home + j, j == 0)
+            multiply(core, j, j == 0)
         step = next_step
         for j in range(PARTS):
             arrived(step[j])
-            multiply(away + j, False)
+            multiply(1 - core, j, False)
 
         before = acc[...]
         hidden = (before / (1.0 + jnp.exp(-before))).astype(jnp.bfloat16)
         affinity = jax.nn.sigmoid(kept[:, 0:1]).astype(jnp.bfloat16).astype(jnp.float32)
         gate = affinity * kept[:, 1:2]
         counts_once = jnp.where(y == 0, 1.0, 0.0)
-        for copy in weight_copies[l][1:]:
-            copy.wait()
-
-        def outcome(k):
-            part = jnp.dot(hidden, down_v[l, k], preferred_element_type=jnp.float32)
+        weight_copies[l][1].wait()
+        fill_tail(tail_down, down_v, l)
+
+        def outcome(side, j):
+            k = side * PARTS + j
+            part = jnp.dot(hidden, chunk(down_v, tail_down, l, side, j), preferred_element_type=jnp.float32)
             marker = aux_ref[l, k].astype(jnp.float32)[1:2] * counts_once
             return gate * (part + marker)
 
         step, next_step = [], []
         for j in range(PARTS):
-            core_out[l, j] = outcome(away + j).astype(jnp.bfloat16)
+            core_out[l, j] = outcome(1 - core, j).astype(jnp.bfloat16)
             step.append([send(core_out.at[l, j], core_in.at[l, j], device(y, z, x, 1 - core))])
         for j in range(PARTS):
-            own = outcome(home + j)
+            own = outcome(core, j)
             arrived(step[j])
             total = (own + core_in[l, j].astype(jnp.float32)).astype(jnp.bfloat16)
             sums[l, j] = total.reshape(ny, nz, 2, half_rows, cols)
@@ -328,38 +353,31 @@
     main = depth // LANES * LANES
     half_rows = 2 * tok
     count = ny * columns * tok
-    slots = jnp.arange(experts, dtype=jnp.int32)
-    place_of = jnp.sum(
-        jnp.where(routes[..., None] == slots, placement[:, None, None, :], 0), axis=3)
-    routed = jnp.any(place_of[..., None] == slots, axis=2).astype(jnp.bfloat16)
-    marks = jnp.pad(routed, ((0, 0), (0, 0), (depth - main, width - depth - experts)))
-    init = jnp.concatenate(
-        [jnp.pad(tokens, ((0, 0), (0, width - depth)))] + [marks[l] for l in range(layers)], axis=1)
-    router_row = jnp.pad(router_weight[:, 0], ((0, 0), (0, width - depth)))
-    own = (jnp.arange(width, dtype=jnp.int32) == depth + lax.axis_index("expert")).astype(jnp.bfloat16)
-    aux = jnp.stack([router_row, jnp.broadcast_to(own, router_row.shape)], axis=1)
-    aux = jnp.pad(aux, ((0, 0), (0, 14), (0, 0)))
-    aux = jnp.transpose(aux.reshape(layers, 16, 2 * PARTS, cols), (0, 2, 1, 3))
-    down_tail = jnp.pad(down_weight[:, 0, :, main:], ((0, 0), (0, 0), (0, width - depth)))
+    top_k = routes.shape[2]
     sends = PARTS * (2 * (nz - 1) + 2 * ny + 2) + 1
     bf16, f32 = jnp.bfloat16, jnp.float32
     in_vmem, anywhere = pl.BlockSpec(memory_space=pltpu.VMEM), pl.BlockSpec(memory_space=pl.ANY)
     return pl.pallas_call(
-        functools.partial(fused_layers, (layers, depth, ny, nz, width, tok)),
+        functools.partial(fused_layers, (layers, depth, ny, nz, width, tok, top_k, experts)),
         out_shape=jax.ShapeDtypeStruct((tok, depth), bf16),
-        in_specs=[in_vmem, in_vmem, anywhere, anywhere, anywhere],
+        in_specs=[in_vmem, in_vmem, in_vmem, in_vmem, anywhere, anywhere],
         out_specs=in_vmem,
         scratch_shapes=[
-            pltpu.VMEM(init.shape, bf16),
+            pltpu.VMEM((layers, tok, width - main), bf16),
+            pltpu.VMEM((tok, depth), bf16),
+            pltpu.VMEM((layers, tok, width - main), bf16),
+            pltpu.VMEM((layers, 2 * PARTS, half_rows, cols), bf16),
+            pltpu.VMEM((layers, block, cols), bf16),
+            pltpu.VMEM((layers, block, cols), bf16),
             pltpu.VMEM((layers, half_rows, width - main), f32),
             pltpu.VMEM((half_rows, width), f32),
             pltpu.VMEM((half_rows, width), f32),
             pltpu.VMEM((layers, 2 * PARTS, half_rows, cols), bf16),
             pltpu.VMEM((layers, 2 * PARTS, ny, nz, 2, half_rows, cols), bf16),
-            pltpu.VMEM((layers, width, block), bf16),
-            pltpu.VMEM((layers, 2 * PARTS, block, cols), bf16),
+            pltpu.VMEM((layers, block, depth), bf16),
+            pltpu.VMEM((layers, block, depth), bf16),
             pltpu.VMEM((count, block), f32),
-            pltpu.VMEM((count, 16), f32),
+            pltpu.VMEM((count, half_rows), f32),
             pltpu.VMEM((layers, PARTS, count, cols), bf16),
             pltpu.VMEM((layers, PARTS, count, cols), bf16),
             pltpu.VMEM((layers, PARTS, ny, nz, 2, half_rows, cols), bf16),
@@ -375,15 +393,15 @@
             pltpu.VMEM((layers, PARTS, nz, half_rows, cols), bf16),
             pltpu.VMEM((layers, PARTS, nz - 1, half_rows, cols), bf16),
             pltpu.VMEM((layers, 2 * PARTS, half_rows, cols), bf16),
-            pltpu.SemaphoreType.DMA((layers, 3 + main // cols)),
-            pltpu.SemaphoreType.DMA,
-            pltpu.SemaphoreType.DMA,
+            pltpu.SemaphoreType.DMA((layers, 2)),
+            pltpu.SemaphoreType.DMA((2,)),
+            pltpu.SemaphoreType.DMA((2,)),
             pltpu.SemaphoreType.DMA((layers, sends)),
             pltpu.SemaphoreType.DMA((layers, sends)),
         ],
         compiler_params=pltpu.CompilerParams(
             collective_id=0, has_side_effects=True, vmem_limit_bytes=VMEM_BYTES),
-    )(init, aux, up_weight, down_weight, down_tail)
+    )(tokens, routes, placement, router_weight[:, 0], jnp.swapaxes(up_weight, 2, 3), down_weight)
 
 
 VMEM_BYTES = 60 << 20
@@ -402,11 +420,11 @@
     main = depth // LANES * LANES
     count = ny * columns * tok
     lanes = -(-block // LANES) * LANES
-    need = layers * 2 * width * (2 * lanes + 4 * count) + 4 * count * (3 * lanes + width // 4)
+    need = layers * 2 * width * (3 * lanes + 4 * count) + 4 * count * (3 * lanes + width // 4)
     return (
         ny > 1 and columns % 4 == 0 and columns > 4 and experts == columns and up_weight.shape[1] == 1
         and tok % 8 == 0 and depth % 16 == 0 and block % 16 == 0
-        and width - main <= width // (2 * PARTS) and need < VMEM_BYTES
+        and depth > width - width // (2 * PARTS) and need < VMEM_BYTES
     )
 
 

time: 96.3 us -> 77.8 us (0.81)
  local copies, waits for them, and re-layouts: 16.8 us -> 2.78 us
  other arithmetic: 2.68 us -> 0 us
  Pallas kernels: 76.1 us -> 74.7 us
    unnamed x2, local copies, waits for them, and re-layouts: 13.2 us -> 2.78 us
    concatenate x1 -> x0, other arithmetic: 1.43 us -> none  [plan_by_kernel(): jnp.concatenate([jnp.pad(tokens, ((0, 0), (0, width - depth)))] + [marks[...]
    pallas_call x1, Pallas kernels: 76.1 us -> 74.7 us  [plan_by_kernel(): pl.pallas_call(functools.partial(fused_layers, (layers, depth, ny, nz, wi...]
    pad x1 -> x0, local copies, waits for them, and re-layouts: 1.06 us -> none  [plan_by_kernel(): jnp.pad(down_weight[:, 0, :, main:], ((0, 0), (0, 0), (0, width - depth)))]
    squeeze x2 -> x0, local copies, waits for them, and re-layouts: 1.02 us -> none  [the longest x1 1.01 us: plan_by_kernel(): down_weight[:, 0, :, main:]]
    reduce_sum x1 -> x0, other arithmetic: 0.98 us -> none  [plan_by_kernel(): jnp.sum(jnp.where(routes[..., None] == slots, placement[:, None, None, :]...]
where the time goes in v2:
time: 77.8 us; the launch traced here: 77.5 us
  Pallas kernels  74.7 us (96%)
  local copies, waits for them, and re-layouts  2.78 us (4%)
    pallas_call x1, Pallas kernels, plan_by_kernel(): pl.pallas_call(functools.partial(fused_layers, (layers, depth, ny, nz, wi...  74.7 us
    unnamed x2, local copies, waits for them, and re-layouts  2.78 us

profile of v2, /device:TPU:1, one launch (start us, length us, event | category | flops | bytes accessed | tf_op | source)
XLA Modules:
  0.0 77.5 jit_solution(7466116800618132413)
XLA Ops:
  0.0 1.4 %copy.7.routes_ref = s32[2,8,4]{2,1,0:T(8,128)} copy(s32[2,8,4]{1,2,0:T(4,128)} %param.7) | data formatting | bytes 512 | tf_op args[1]
  1.4 74.7 %shard_map.64 = bf16[8,2880]{1,0:T(8,128)(2,1)} custom-call(bf16[8,2880]{1,0:T(8,128)(2,1)} %tokens_ref.1, s32[2,8,4]{2,1,0:T(8,128)} %copy.7.routes_ref, s32[2,16]{1,0:T(2,128)} %placement_ref.1, bf16[2,2880]{1,0:T(2,128)(2,1)} %bitcast.3, bf16[2,1,720,2880]{3,2,1,0:T(8,128)(2,1)} %bitcast.2, bf16[2,1,720,2880]{3,2,1,0:T(8,128)(2,1)} %down_hbm.1), custom_call_target="tpu_custom_call" | custom-call | tf_op jit(solution)/shard_map/pallas_call | solution.py:360
  76.1 1.4 %copy.9 = bf16[8,2880]{1,0:T(8,128)(2,1)} copy(bf16[8,2880]{1,0:T(8,128)(2,1)} %shard_map.64) | data formatting | bytes 92160
